TPU v7x, 128 devices: a whole 4x4x4 slice. The times are simulated.
128 devices in a mesh: grp: 4 (over z), tile: 32 (over x, y, core).
Axes of the slice: x: 4, y: 4, z: 4, core: 2. Of those that a mesh axis runs over, the one named last changes fastest.
Arguments:
- noise: bfloat16 [16, 3, 2048, 2048], P('grp', None, 'tile'), may hold values from -6 to 6
- stress: float32 [6, 2048, 2048], P(None, 'tile', 'grp'), as said below
- timescale: float32 [2048, 2048], P('tile', 'grp'), may hold values from 3 to 256
- mean_inflow: float32 [2048, 2048], P('tile', 'grp'), may hold values from 0.5 to 1.5
- courant: float32 [2048, 2048], P('tile', 'grp'), may hold values from 0.2 to 0.9
- prior_state: float32 [3, 2048, 2048], P(None, 'tile', 'grp'), may hold values from -6 to 6
- field: float32 [3, 8, 2048, 2048], P(None, None, 'tile', 'grp'), may hold values from -6 to 6
Outputs:
- inflow: bfloat16 [16, 3, 2048, 2048], P(None, None, 'tile', 'grp')
- field_out: float32 [3, 8, 2048, 2048], P(None, None, 'tile', 'grp')
Inputs may be any that keep to these rules, and one draw needn't show every extreme that they name: stress holds, per cell, R11, R21, R22, R31, R32, R33 of a symmetric positive definite tensor whose Cholesky factor has diagonal entries of 0.3 or more.
All inputs are finite; a program needn't handle non-finite values.
Results may differ from a plain program's by a relative error of at most 0.0085.
Values may be sent and summed in bfloat16 or wider, within the bound.
A program may use at most 128 MiB of HBM per device.

v0:
```python
import math
import jax
import jax.numpy as jnp
from jax import lax
from jax.sharding import PartitionSpec as P

LS = 2
FW = 4


def padded_2(value, sides, width, wrap):
    for axis, dim in sides:
        devices, length = (lax.axis_size(axis), value.shape[dim])
        up = [(i, (i + 1) % devices) for i in range(devices if wrap else devices - 1)]
        down = [(j, i) for i, j in up]
        last = lax.slice_in_dim(value, length - width, length, axis=dim)
        initial = lax.slice_in_dim(value, 0, width, axis=dim)
        before = lax.ppermute(last, axis, up)
        after = lax.ppermute(initial, axis, down)
        value = jnp.concatenate([before, value, after], axis=dim)
    return value


def filter_taps():
    offsets = jnp.arange(-FW, FW + 1).astype(jnp.float32)
    raw = jnp.exp(-math.pi * offsets * offsets / (2.0 * LS * LS))
    return (raw / jnp.sqrt(jnp.sum(raw * raw))).astype(jnp.bfloat16)


def band_matrix(rows, taps):
    width = taps.shape[0]
    distance = jnp.arange(rows + width - 1)[None, :] - jnp.arange(rows)[:, None]
    picks = distance[:, :, None] == jnp.arange(width)[None, None, :]
    return jnp.sum(jnp.where(picks, taps.astype(jnp.float32), 0.0), axis=2).astype(jnp.bfloat16)


def filter_last(padded, taps):
    width = taps.shape[0]
    length = padded.shape[-1] - width + 1
    block = math.gcd(length, 128)
    weights = band_matrix(block, taps)
    windows = jnp.stack(
        [
            lax.slice_in_dim(padded, start, start + block + width - 1, axis=padded.ndim - 1)
            for start in range(0, length, block)
        ],
        axis=-2,
    )
    result = jnp.einsum("...kw,bw->...kb", windows, weights, preferred_element_type=jnp.float32)
    return result.reshape(result.shape[:-2] + (length,))


def filter_rows(padded, taps):
    rows = padded.shape[2] - taps.shape[0] + 1
    weights = band_matrix(rows, taps)
    return jnp.einsum("ij,pcjz->pciz", weights, padded, preferred_element_type=jnp.float32)


def cholesky_cells(stress):
    first_diag = jnp.sqrt(stress[0])
    second_low = stress[1] / first_diag
    second_diag = jnp.sqrt(stress[2] - second_low * second_low)
    third_low = stress[3] / first_diag
    third_mid = (stress[4] - second_low * third_low) / second_diag
    third_diag = jnp.sqrt(stress[5] - third_low * third_low - third_mid * third_mid)
    return (first_diag, second_low, second_diag, third_low, third_mid, third_diag)


def velocity_of(state, factors, mean_inflow):
    first_diag, second_low, second_diag, third_low, third_mid, third_diag = factors
    return jnp.stack(
        [
            mean_inflow + first_diag * state[0],
            second_low * state[0] + second_diag * state[1],
            third_low * state[0] + third_mid * state[1] + third_diag * state[2],
        ]
    )


def march(current, courant, velocity):
    upstream = jnp.concatenate([velocity[:, None], current[:, :-1]], axis=1)
    return (1.0 - courant) * current + courant * upstream


def tile_chain(filtered, stress, timescale, mean_inflow, courant, prior_state, field):
    decay = jnp.exp(-math.pi / (2.0 * timescale))
    gain = jnp.sqrt(1.0 - decay * decay)
    factors = cholesky_cells(stress)

    def advance(carry, plane):
        state, current = carry
        state = decay * state + gain * plane
        velocity = velocity_of(state, factors, mean_inflow)
        return ((state, march(current, courant, velocity)), velocity.astype(jnp.bfloat16))

    (state, result), inflow = lax.scan(advance, (prior_state, field), filtered)
    return (inflow, result)


def body(noise, stress, timescale, mean_inflow, courant, prior_state, field):
    taps = filter_taps()
    flipped = jnp.swapaxes(noise, 2, 3)
    tiles = lax.all_to_all(
        lax.all_to_all(flipped, "tile", split_axis=2, concat_axis=3, tiled=True),
        "grp",
        split_axis=3,
        concat_axis=0,
        tiled=True,
    )
    banded = padded_2(tiles, (("grp", 3),), FW, False)
    widened = padded_2(banded, (("tile", 2),), FW, True)
    span = filter_rows(widened, taps).astype(jnp.bfloat16)
    filtered = filter_last(span, taps)
    inflow, result = tile_chain(
        filtered, stress, timescale, mean_inflow, courant, prior_state, field
    )
    return (inflow, result)


def solution(mesh):
    placed = (
        P("grp", None, "tile", None),
        P(None, "tile", "grp"),
        P("tile", "grp"),
        P("tile", "grp"),
        P("tile", "grp"),
        P(None, "tile", "grp"),
        P(None, None, "tile", "grp"),
    )
    return jax.shard_map(
        body,
        mesh=mesh,
        in_specs=placed,
        out_specs=(P(None, None, "tile", "grp"), P(None, None, "tile", "grp")),
        check_vma=False,
    )
```

profile of v0, /device:TPU:63, one launch (start us, length us, event | category | flops | bytes accessed | tf_op | source)
XLA Modules:
  0.0 310.5 jit_solution(12647594609920412347)
XLA Ops:
  0.6 1.9 copy-done.7
  2.5 7.1 %copy.41 = bf16[4,3,64,2048]{2,0,1,3:T(4,128)(2,1)} copy(bf16[4,3,64,2048]{3,2,1,0:T(8,128)(2,1)S(1)} %copy-done.7) | data formatting | bytes 6291456 | tf_op args[0]
  9.6 7.7 %bitcast_bitcast_fusion = bf16[2048,3,4,64]{3,2,1,0:T(4,128)(2,1)} fusion(bf16[4,3,64,2048]{2,0,1,3:T(4,128)(2,1)} %copy.41), kind=kLoop, calls=%fused_computation.73 | loop fusion | bytes 6291456
  17.3 7.5 %reshape.107 = bf16[32,2,24576]{2,1,0:T(2,128)(2,1)S(1)} reshape(bf16[2048,3,4,64]{3,2,1,0:T(4,128)(2,1)} %bitcast_bitcast_fusion) | data formatting | bytes 6291456
  24.8 43.9 %all_to_all.36 = bf16[32,2,24576]{2,1,0:T(2,128)(2,1)} all-to-all(bf16[32,2,24576]{2,1,0:T(2,128)(2,1)S(1)} %reshape.107), channel_id=1, replica_groups=mesh['grp'=4,'tile'=32] {'tile'}, dimensions={0} | all-to-all | bytes 6291456 | tf_op jit(solution)/shard_map/all_to_all | solution.py:104
  68.7 8.7 %reshape.108 = bf16[2048,3,4,64]{3,2,1,0:T(4,128)(2,1)} reshape(bf16[32,2,24576]{2,1,0:T(2,128)(2,1)} %all_to_all.36) | data formatting | bytes 6291456
  77.4 9.5 %copy.65 = bf16[4,3,32,64,64]{4,2,3,1,0:T(8,128)(2,1)} copy(bf16[4,3,32,64,64]{4,0,1,3,2:T(4,128)(2,1)} %bitcast.127) | data formatting | bytes 6291456 | tf_op jit(solution)/shard_map/all_to_all | solution.py:104
  86.9 11.8 %copy.54 = bf16[4,3,64,32,64]{2,0,1,4,3:T(4,128)(2,1)} copy(bf16[4,3,64,32,64]{4,3,2,1,0:T(8,128)(2,1)} %bitcast.128) | data formatting | bytes 6291456 | tf_op jit(solution)/shard_map/all_to_all | solution.py:104
  98.7 7.7 %reshape.109 = bf16[4,2,196608]{2,1,0:T(2,128)(2,1)} reshape(bf16[2048,3,4,64]{3,2,1,0:T(4,128)(2,1)} %bitcast.129) | data formatting | bytes 6291456
  106.5 5.0 %all-to-all-start.1 = ((bf16[4,2,196608]{2,1,0:T(2,128)(2,1)}), bf16[4,2,196608]{2,1,0:T(2,128)(2,1)S(1)}, u32[]{:S(2)}, u32[]{:S(2)}) async-start(bf16[4,2,196608]{2,1,0:T(2,128)(2,1)} %reshape.109), calls=%async_computation.1 | async-start | bytes 6291456 | tf_op jit(solution)/shard_map/all_to_all | solution.py:103
  112.9 2.2 fusion.24
  115.8 1.6 fusion.26
  117.4 30.1 %all-to-all-done.1 = bf16[4,2,196608]{2,1,0:T(2,128)(2,1)S(1)} async-done(((bf16[4,2,196608]{2,1,0:T(2,128)(2,1)}), bf16[4,2,196608]{2,1,0:T(2,128)(2,1)S(1)}, u32[]{:S(2)}, u32[]{:S(2)}) %all-to-all-start.1) | async-done | bytes 3145760 | tf_op jit(solution)/shard_map/all_to_all | solution.py:103
  147.5 5.3 %reshape.110 = bf16[2048,3,4,64]{3,2,1,0:T(4,128)(2,1)} reshape(bf16[4,2,196608]{2,1,0:T(2,128)(2,1)S(1)} %all-to-all-done.1) | data formatting | bytes 6291456
  152.8 8.3 %copy.45 = bf16[4,4,3,64,512]{4,3,2,1,0:T(8,128)(2,1)S(1)} copy(bf16[4,4,3,64,512]{3,1,2,4,0:T(4,128)(2,1)} %bitcast.130) | data formatting | bytes 6291456 | tf_op jit(solution)/shard_map/all_to_all | solution.py:103
  161.1 1.5 fusion.38
  162.6 1.5 copy.46
  164.1 1.5 copy.47
  165.7 3.1 collective-permute-start.1
  168.8 2.4 collective-permute-start
  171.3 2.3 collective-permute-done
  176.1 1.8 pad_maximum_fusion.3
  177.9 5.7 %collective-permute-start.2 = (bf16[16,3,4,520]{3,2,1,0:T(4,128)(2,1)S(1)}, bf16[16,3,4,520]{3,2,1,0:T(4,128)(2,1)S(1)}, u32[]{:S(2)}, u32[]{:S(2)}) collective-permute-start(bf16[16,3,4,520]{3,2,1,0:T(4,128)(2,1)S(1)} %get-tuple-element.126), channel_id=1, source_target_pairs={{0,1},{1,2},{2,3},{3,4},{4,5},{5,6},{6,7},{7,8},{8,9},{9,10},{10,1... | collective-permute-start | bytes 599048 | tf_op jit(solution)/shard_map/ppermute | solution.py:18
  183.6 1.6 sqrt_bitcast_fusion
  185.2 1.5 collective-permute-done.2
  186.7 5.8 %collective-permute-done.3 = bf16[16,3,4,520]{3,2,1,0:T(4,128)(2,1)S(1)} collective-permute-done((bf16[16,3,4,520]{3,2,1,0:T(4,128)(2,1)S(1)}, bf16[16,3,4,520]{3,2,1,0:T(4,128)(2,1)S(1)}, u32[]{:S(2)}, u32[]{:S(2)}) %collective-permute-start.3) | collective-permute-done | bytes 199712 | tf_op jit(solution)/shard_map/ppermute | solution.py:19
  192.5 4.2 %convert_bitcast_fusion.3 = bf16[16,3,64,520]{3,2,1,0:T(8,128)(2,1)S(1)} fusion(bf16[16,3,4,520]{3,2,1,0:T(4,128)(2,1)S(1)} %collective-permute-done.3, bf16[16,3,64,4]{3,2,1,0:T(8,128)(2,1)S(1)} %copy-done.6, bf16[16,3,64,512]{3,2,1,0:T(8,128)(2,1)S(1)} %bitcast.133, bf16[16,3,64,4]{3,2,1,0:T(8,128)(2,1)S(1)} %copy-done.5, ...), kind=kOutput, calls=%fused_computation.35 | convolution fusion | flops 249600000 | bytes 6798336 | tf_op jit(solution)/shard_map/ij,pcjz->pciz/dot_general | solution.py:56
  197.6 2.6 fusion.18
  200.2 3.5 %copy.64 = f32[16,3,4,8,8,128]{5,4,2,3,1,0:T(8,128)} copy(f32[16,3,4,8,8,128]{5,4,3,2,1,0:T(8,128)S(1)} %fusion.18) | data formatting | bytes 12582912 | tf_op jit(solution)/shard_map/reshape | solution.py:50
  203.7 105.1 %while.14 = (s32[]{:T(128)}, f32[3,64,512]{2,1,0:T(8,128)S(1)}, f32[3,8,64,512]{3,2,1,0:T(8,128)S(1)}, bf16[16,3,64,512]{3,2,1,0:T(8,128)(2,1)}, f32[64,512]{1,0...) while((s32[]{:T(128)}, f32[3,64,512]{2,1,0:T(8,128)S(1)}, ...), condition=%wide.region_4.5_spmd, body=%wide.region_3.4_spmd.sunk | while | flops 4685826 | bytes 20512960 | solution.py:96
  204.6 1.3 fusion.41
  205.9 1.4 convert_bitcast_fusion.5
  208.2 1.4 fusion.42
  212.5 1.4 convert_bitcast_fusion.5
  214.7 1.4 fusion.42
  219.0 1.4 convert_bitcast_fusion.5
  221.3 1.4 fusion.42
  225.6 1.4 convert_bitcast_fusion.5
  227.9 1.4 fusion.42
  232.2 1.4 convert_bitcast_fusion.5
  234.5 1.4 fusion.42
  238.7 1.4 convert_bitcast_fusion.5
  241.0 1.4 fusion.42
  245.3 1.4 convert_bitcast_fusion.5
  247.6 1.4 fusion.42
  251.9 1.4 convert_bitcast_fusion.5
  254.2 1.4 fusion.42
  258.4 1.4 convert_bitcast_fusion.5
  260.7 1.4 fusion.42
  265.0 1.4 convert_bitcast_fusion.5
  267.3 1.4 fusion.42
  271.6 1.4 convert_bitcast_fusion.5
  273.9 1.4 fusion.42
  278.2 1.4 convert_bitcast_fusion.5
  280.4 1.4 fusion.42
  284.7 1.4 convert_bitcast_fusion.5
  287.0 1.4 fusion.42
  291.3 1.4 convert_bitcast_fusion.5
  293.6 1.4 fusion.42
  297.9 1.4 convert_bitcast_fusion.5
  300.2 1.4 fusion.42
  304.4 1.4 convert_bitcast_fusion.5
  306.7 1.4 fusion.42
  308.8 1.7 copy-done
  (137 shorter events, 64.1 us)
Async XLA Ops:
  0.6 1.9 copy-start.7
  106.5 6.5 %copy-start.8 = (f32[64,512]{1,0:T(8,128)S(1)}, f32[64,512]{1,0:T(8,128)}, u32[]{:S(2)}) copy-start(f32[64,512]{1,0:T(8,128)} %param.11) | copy-start | bytes 393220
  106.5 41.0 %all-to-all-start.1 = ((bf16[4,2,196608]{2,1,0:T(2,128)(2,1)}), bf16[4,2,196608]{2,1,0:T(2,128)(2,1)S(1)}, u32[]{:S(2)}, u32[]{:S(2)}) async-start(bf16[4,2,196608]{2,1,0:T(2,128)(2,1)} %reshape.109), calls=%async_computation.1 | async-start | bytes 6291456 | tf_op jit(solution)/shard_map/all_to_all | solution.py:103
  115.1 0.7 copy-start.4
  165.7 9.2 %collective-permute-start.1 = (bf16[16,3,64,4]{2,0,3,1:T(8,128)(2,1)S(1)}, bf16[16,3,64,4]{2,0,3,1:T(8,128)(2,1)S(1)}, u32[]{:S(2)}, u32[]{:S(2)}) collective-permute-start(bf16[16,3,64,4]{2,0,3,1:T(8,128)(2,1)S(1)} %copy.47), channel_id=1, source_target_pairs={{32,0},{64,32},{96,64},{33,1},{65,33},{97,65},{34,2},{66,34},{98,6... | collective-permute-start | bytes 73736 | tf_op jit(solution)/shard_map/ppermute | solution.py:19
  168.8 4.8 %collective-permute-start = (bf16[16,3,64,4]{2,0,3,1:T(8,128)(2,1)S(1)}, bf16[16,3,64,4]{2,0,3,1:T(8,128)(2,1)S(1)}, u32[]{:S(2)}, u32[]{:S(2)}) collective-permute-start(bf16[16,3,64,4]{2,0,3,1:T(8,128)(2,1)S(1)} %copy.46), channel_id=1, source_target_pairs={{0,32},{32,64},{64,96},{1,33},{33,65},{65,97},{2,34},{34,66},{66,9... | collective-permute-start | bytes 73736 | tf_op jit(solution)/shard_map/ppermute | solution.py:18
  176.1 16.4 %copy-start.5 = (bf16[16,3,64,4]{3,2,1,0:T(8,128)(2,1)S(1)}, bf16[16,3,64,4]{3,2,1,0:T(8,128)(2,1)}, u32[]{:S(2)}) copy-start(bf16[16,3,64,4]{3,2,1,0:T(8,128)(2,1)} %copy.48) | copy-start | bytes 73732
  176.1 16.4 %copy-start.6 = (bf16[16,3,64,4]{3,2,1,0:T(8,128)(2,1)S(1)}, bf16[16,3,64,4]{3,2,1,0:T(8,128)(2,1)}, u32[]{:S(2)}) copy-start(bf16[16,3,64,4]{3,2,1,0:T(8,128)(2,1)} %copy.49) | copy-start | bytes 73732
  177.9 8.8 %collective-permute-start.2 = (bf16[16,3,4,520]{3,2,1,0:T(4,128)(2,1)S(1)}, bf16[16,3,4,520]{3,2,1,0:T(4,128)(2,1)S(1)}, u32[]{:S(2)}, u32[]{:S(2)}) collective-permute-start(bf16[16,3,4,520]{3,2,1,0:T(4,128)(2,1)S(1)} %get-tuple-element.126), channel_id=1, source_target_pairs={{0,1},{1,2},{2,3},{3,4},{4,5},{5,6},{6,7},{7,8},{8,9},{9,10},{10,1... | collective-permute-start | bytes 599048 | tf_op jit(solution)/shard_map/ppermute | solution.py:18
  183.6 8.9 %collective-permute-start.3 = (bf16[16,3,4,520]{3,2,1,0:T(4,128)(2,1)S(1)}, bf16[16,3,4,520]{3,2,1,0:T(4,128)(2,1)S(1)}, u32[]{:S(2)}, u32[]{:S(2)}) collective-permute-start(bf16[16,3,4,520]{3,2,1,0:T(4,128)(2,1)S(1)} %get-tuple-element.127), channel_id=1, source_target_pairs={{1,0},{2,1},{3,2},{4,3},{5,4},{6,5},{7,6},{8,7},{9,8},{10,9},{11,1... | collective-permute-start | bytes 599048 | tf_op jit(solution)/shard_map/ppermute | solution.py:19
  200.2 3.5 %copy-start.1 = (f32[3,8,64,512]{3,2,1,0:T(8,128)S(1)}, f32[3,8,64,512]{3,2,1,0:T(8,128)}, u32[]{:S(2)}) copy-start(f32[3,8,64,512]{3,2,1,0:T(8,128)} %param.15) | copy-start | bytes 9437188
  200.2 3.5 %copy-start.2 = (f32[3,64,512]{2,1,0:T(8,128)S(1)}, f32[3,64,512]{2,1,0:T(8,128)}, u32[]{:S(2)}) copy-start(f32[3,64,512]{2,1,0:T(8,128)} %param.14) | copy-start | bytes 1179652
  207.3 0.9 copy-start.3
  213.8 0.9 copy-start.3
  220.4 0.9 copy-start.3
  227.0 0.9 copy-start.3
  233.6 0.9 copy-start.3
  240.1 0.9 copy-start.3
  246.7 0.9 copy-start.3
  253.3 0.9 copy-start.3
  259.8 0.9 copy-start.3
  266.4 0.9 copy-start.3
  273.0 0.9 copy-start.3
  279.5 0.9 copy-start.3
  286.1 0.9 copy-start.3
  292.7 0.9 copy-start.3
  299.3 0.9 copy-start.3
  305.8 0.9 copy-start.3
  308.8 1.7 copy-start
where the time goes:
time: 313 us; the launch traced here: 310 us
  local copies, waits for them, and re-layouts  105 us (34%)
  other arithmetic  97.3 us (31%)
  blocking collectives  43.9 us (14%)
  waiting for transfers between devices  39.8 us (13%)
  starting transfers between devices  16.1 us (5%)
  matrix products  6.73 us (2%)
    unnamed x22, local copies, waits for them, and re-layouts  48.3 us
    all_to_all x1, blocking collectives, body(): lax.all_to_all(flipped, 'tile', split_axis=2, concat_axis=3, tiled=True)  43.9 us
    all_to_all x1, waiting for transfers between devices, body(): lax.all_to_all(lax.all_to_all(flipped, 'tile', split_axis=2, concat_axis=...  30.1 us
    another operation x16, other arithmetic, velocity_of(): jnp.stack([mean_inflow + first_diag * state[0], second_low * state[0] + s...  22.1 us
    add x16, other arithmetic, march(): return (1.0 - courant) * current + courant * upstream  22.1 us
    all_to_all x2, local copies, waits for them, and re-layouts, body(): lax.all_to_all(flipped, 'tile', split_axis=2, concat_axis=3, tiled=True)  21.3 us
    add x16, other arithmetic, advance(): state = decay * state + gain * plane  20.4 us
    sub x16, other arithmetic, march(): return (1.0 - courant) * current + courant * upstream  14.6 us
  transfers between devices with their start and end apart: 5, of which 4 were waited for; matrix products, arithmetic and copies ran while one was open for 2% of the time, Pallas kernels for 0%

commit v1 on v0

--- a/solution.py
+++ b/solution.py
@@ -101,7 +101,12 @@
     taps = filter_taps()
     flipped = jnp.swapaxes(noise, 2, 3)
     tiles = lax.all_to_all(
-        lax.all_to_all(flipped, "tile", split_axis=2, concat_axis=3, tiled=True),
+        jnp.concatenate(
+            lax.all_to_all(
+                jnp.stack(jnp.split(flipped, lax.axis_size("tile"), axis=2)), "tile", 0, 0
+            ),
+            axis=3,
+        ),
         "grp",
         split_axis=3,
         concat_axis=0,

time: 313 us -> 289 us (0.923)
  local copies, waits for them, and re-layouts: 105 us -> 78.4 us
    all_to_all x3 -> x1, local copies, waits for them, and re-layouts: 29.5 us -> 8.27 us  [body(): lax.all_to_all(jnp.concatenate(lax.all_to_all(jnp.stack(jnp.split(flipped...]
    reshape x0 -> x2, local copies, waits for them, and re-layouts: none -> 12.8 us  [body(): jnp.concatenate(lax.all_to_all(jnp.stack(jnp.split(flipped, lax.axis_size...]
    while x32, local copies, waits for them, and re-layouts: 9.15 us -> 0.06 us
    unnamed x22 -> x49, local copies, waits for them, and re-layouts: 48.3 us -> 39.6 us
  transfers between devices with their start and end apart: 5 -> 5, of which waited for: 4 -> 4; matrix products, arithmetic and copies ran while one was open for 2% -> 3% of each run, Pallas kernels for 0% -> 0%
where the time goes in v1:
time: 289 us; the launch traced here: 287 us
  other arithmetic  98.4 us (34%)
  local copies, waits for them, and re-layouts  78.4 us (27%)
  blocking collectives  43.9 us (15%)
  waiting for transfers between devices  40 us (14%)
  starting transfers between devices  16 us (6%)
  matrix products  7.9 us (3%)
    all_to_all x1, blocking collectives, body(): lax.all_to_all(jnp.stack(jnp.split(flipped, lax.axis_size('tile'), axis=2...  43.9 us
    unnamed x49, local copies, waits for them, and re-layouts  39.6 us
    all_to_all x1, waiting for transfers between devices, body(): lax.all_to_all(jnp.concatenate(lax.all_to_all(jnp.stack(jnp.split(flipped...  30.1 us
    another operation x16, other arithmetic, velocity_of(): jnp.stack([mean_inflow + first_diag * state[0], second_low * state[0] + s...  22.1 us
    add x16, other arithmetic, march(): return (1.0 - courant) * current + courant * upstream  22.1 us
    add x16, other arithmetic, advance(): state = decay * state + gain * plane  20.4 us
    sub x16, other arithmetic, march(): return (1.0 - courant) * current + courant * upstream  15.8 us
    reshape x2, local copies, waits for them, and re-layouts, body(): jnp.concatenate(lax.all_to_all(jnp.stack(jnp.split(flipped, lax.axis_size...  12.8 us
  transfers between devices with their start and end apart: 5, of which 4 were waited for; matrix products, arithmetic and copies ran while one was open for 3% of the time, Pallas kernels for 0%

profile of v1, /device:TPU:63, one launch (start us, length us, event | category | flops | bytes accessed | tf_op | source)
XLA Modules:
  0.0 286.9 jit_solution(739546389769858706)
XLA Ops:
  0.6 1.9 copy-done.4
  6.3 2.6 copy-done.5
  8.9 7.5 %reshape.115 = bf16[32,2,24576]{2,1,0:T(2,128)(2,1)S(1)} reshape(bf16[32,4,3,64,64]{4,3,2,1,0:T(8,128)(2,1)} %bitcast.290) | data formatting | bytes 6291456
  16.5 43.9 %all_to_all.23 = bf16[32,2,24576]{2,1,0:T(2,128)(2,1)} all-to-all(bf16[32,2,24576]{2,1,0:T(2,128)(2,1)S(1)} %reshape.115), channel_id=1, replica_groups=mesh['grp'=4,'tile'=32] {'tile'}, dimensions={0} | all-to-all | bytes 6291456 | tf_op jit(solution)/shard_map/all_to_all | solution.py:105
  60.4 8.7 %reshape.116 = bf16[32,4,3,64,64]{4,3,2,1,0:T(8,128)(2,1)} reshape(bf16[32,2,24576]{2,1,0:T(2,128)(2,1)} %all_to_all.23) | data formatting | bytes 6291456
  69.1 4.3 %bitcast_bitcast_fusion = bf16[4,3,64,32,64]{2,4,1,0,3:T(8,128)(2,1)S(1)} fusion(bf16[32,4,3,64,64]{4,3,2,1,0:T(8,128)(2,1)} %reshape.116), kind=kLoop, calls=%fused_computation.136 | loop fusion | bytes 6291456 | tf_op jit(solution)/shard_map/reshape | solution.py:104
  73.4 8.5 %copy.51 = bf16[4,3,64,32,64]{2,0,1,4,3:T(4,128)(2,1)} copy(bf16[4,3,64,32,64]{2,4,1,0,3:T(8,128)(2,1)S(1)} %bitcast_bitcast_fusion) | data formatting | bytes 6291456 | tf_op jit(solution)/shard_map/reshape | solution.py:104
  81.9 7.8 %reshape.117 = bf16[4,2,196608]{2,1,0:T(2,128)(2,1)} reshape(bf16[2048,3,4,64]{3,2,1,0:T(4,128)(2,1)} %bitcast.252) | data formatting | bytes 6291456
  89.6 4.9 %all-to-all-start.1 = ((bf16[4,2,196608]{2,1,0:T(2,128)(2,1)}), bf16[4,2,196608]{2,1,0:T(2,128)(2,1)S(1)}, u32[]{:S(2)}, u32[]{:S(2)}) async-start(bf16[4,2,196608]{2,1,0:T(2,128)(2,1)} %reshape.117), calls=%async_computation.1 | async-start | bytes 6291456 | tf_op jit(solution)/shard_map/all_to_all | solution.py:103
  96.0 2.2 fusion.56
  98.8 1.6 fusion.58
  100.4 30.1 %all-to-all-done.1 = bf16[4,2,196608]{2,1,0:T(2,128)(2,1)S(1)} async-done(((bf16[4,2,196608]{2,1,0:T(2,128)(2,1)}), bf16[4,2,196608]{2,1,0:T(2,128)(2,1)S(1)}, u32[]{:S(2)}, u32[]{:S(2)}) %all-to-all-start.1) | async-done | bytes 3145760 | tf_op jit(solution)/shard_map/all_to_all | solution.py:103
  130.6 5.3 %reshape.118 = bf16[2048,3,4,64]{3,2,1,0:T(4,128)(2,1)} reshape(bf16[4,2,196608]{2,1,0:T(2,128)(2,1)S(1)} %all-to-all-done.1) | data formatting | bytes 6291456
  135.8 8.3 %copy.42 = bf16[4,4,3,64,512]{4,3,2,1,0:T(8,128)(2,1)S(1)} copy(bf16[4,4,3,64,512]{3,1,2,4,0:T(4,128)(2,1)} %bitcast.253) | data formatting | bytes 6291456 | tf_op jit(solution)/shard_map/all_to_all | solution.py:103
  144.1 1.5 fusion.70
  145.7 1.5 copy.43
  147.2 1.5 copy.44
  148.7 3.3 %collective-permute-start.1 = (bf16[16,3,64,4]{2,0,3,1:T(8,128)(2,1)S(1)}, bf16[16,3,64,4]{2,0,3,1:T(8,128)(2,1)S(1)}, u32[]{:S(2)}, u32[]{:S(2)}) collective-permute-start(bf16[16,3,64,4]{2,0,3,1:T(8,128)(2,1)S(1)} %copy.44), channel_id=1, source_target_pairs={{32,0},{64,32},{96,64},{33,1},{65,33},{97,65},{34,2},{66,34},{98,6... | collective-permute-start | bytes 73736 | tf_op jit(solution)/shard_map/ppermute | solution.py:19
  152.0 2.2 collective-permute-start
  154.3 2.5 collective-permute-done
  159.4 1.7 pad_maximum_fusion.3
  161.1 5.7 %collective-permute-start.2 = (bf16[16,3,4,520]{3,2,1,0:T(4,128)(2,1)S(1)}, bf16[16,3,4,520]{3,2,1,0:T(4,128)(2,1)S(1)}, u32[]{:S(2)}, u32[]{:S(2)}) collective-permute-start(bf16[16,3,4,520]{3,2,1,0:T(4,128)(2,1)S(1)} %get-tuple-element.126), channel_id=1, source_target_pairs={{0,1},{1,2},{2,3},{3,4},{4,5},{5,6},{6,7},{7,8},{8,9},{9,10},{10,1... | collective-permute-start | bytes 599048 | tf_op jit(solution)/shard_map/ppermute | solution.py:18
  166.7 1.6 sqrt_bitcast_fusion
  168.3 1.6 collective-permute-done.2
  169.9 5.8 %collective-permute-done.3 = bf16[16,3,4,520]{3,2,1,0:T(4,128)(2,1)S(1)} collective-permute-done((bf16[16,3,4,520]{3,2,1,0:T(4,128)(2,1)S(1)}, bf16[16,3,4,520]{3,2,1,0:T(4,128)(2,1)S(1)}, u32[]{:S(2)}, u32[]{:S(2)}) %collective-permute-start.3) | collective-permute-done | bytes 199712 | tf_op jit(solution)/shard_map/ppermute | solution.py:19
  175.7 5.3 %convert_bitcast_fusion.3 = bf16[16,3,64,520]{3,2,1,0:T(8,128)(2,1)S(1)} fusion(bf16[16,3,4,520]{3,2,1,0:T(4,128)(2,1)S(1)} %collective-permute-done.3, bf16[16,3,64,4]{3,2,1,0:T(8,128)(2,1)} %copy.46, bf16[16,3,64,512]{3,2,1,0:T(8,128)(2,1)S(1)} %bitcast.256, bf16[16,3,64,4]{3,2,1,0:T(8,128)(2,1)} %copy.45, ...), kind=kOutput, calls=%fused_computation.34 | convolution fusion | flops 249600000 | bytes 6798336 | tf_op jit(solution)/shard_map/ij,pcjz->pciz/dot_general | solution.py:56
  181.9 2.6 fusion.18
  184.5 3.5 %copy.61 = f32[16,3,4,8,8,128]{5,4,2,3,1,0:T(8,128)} copy(f32[16,3,4,8,8,128]{5,4,3,2,1,0:T(8,128)S(1)} %fusion.18) | data formatting | bytes 12582912 | tf_op jit(solution)/shard_map/reshape | solution.py:50
  188.0 97.2 %while.14 = (s32[]{:T(128)}, f32[3,64,512]{2,1,0:T(8,128)S(1)}, f32[3,8,64,512]{3,2,1,0:T(8,128)S(1)}, bf16[16,3,64,512]{3,2,1,0:T(8,128)(2,1)}, f32[64,512]{1,0...) while((s32[]{:T(128)}, f32[3,64,512]{2,1,0:T(8,128)S(1)}, ...), condition=%wide.region_4.5_spmd, body=%wide.region_3.4_spmd.sunk | while | flops 4685826 | bytes 20512960 | solution.py:96
  189.0 1.3 fusion.73
  190.3 1.4 convert_bitcast_fusion.5
  192.0 1.4 fusion.74
  195.1 1.3 fusion.73
  196.3 1.4 convert_bitcast_fusion.5
  198.1 1.4 fusion.74
  202.4 1.4 convert_bitcast_fusion.5
  204.1 1.4 fusion.74
  208.5 1.4 convert_bitcast_fusion.5
  210.2 1.4 fusion.74
  214.6 1.4 convert_bitcast_fusion.5
  216.3 1.4 fusion.74
  220.6 1.4 convert_bitcast_fusion.5
  222.4 1.4 fusion.74
  226.7 1.4 convert_bitcast_fusion.5
  228.4 1.4 fusion.74
  232.8 1.4 convert_bitcast_fusion.5
  234.5 1.4 fusion.74
  238.9 1.4 convert_bitcast_fusion.5
  240.6 1.4 fusion.74
  245.0 1.4 convert_bitcast_fusion.5
  246.7 1.4 fusion.74
  251.0 1.4 convert_bitcast_fusion.5
  252.8 1.4 fusion.74
  257.1 1.4 convert_bitcast_fusion.5
  258.8 1.4 fusion.74
  263.2 1.4 convert_bitcast_fusion.5
  264.9 1.4 fusion.74
  269.3 1.4 convert_bitcast_fusion.5
  271.0 1.4 fusion.74
  275.3 1.4 convert_bitcast_fusion.5
  277.1 1.4 fusion.74
  281.4 1.4 convert_bitcast_fusion.5
  283.1 1.4 fusion.74
  285.2 1.7 copy-done
  (165 shorter events, 58.4 us)
Async XLA Ops:
  0.6 1.9 copy-start.4
  6.3 2.7 copy-start.5
  81.9 14.1 %copy-start.7 = (f32[64,512]{1,0:T(8,128)S(1)}, f32[64,512]{1,0:T(8,128)}, u32[]{:S(2)}) copy-start(f32[64,512]{1,0:T(8,128)} %param.11) | copy-start | bytes 393220
  89.6 40.9 %all-to-all-start.1 = ((bf16[4,2,196608]{2,1,0:T(2,128)(2,1)}), bf16[4,2,196608]{2,1,0:T(2,128)(2,1)S(1)}, u32[]{:S(2)}, u32[]{:S(2)}) async-start(bf16[4,2,196608]{2,1,0:T(2,128)(2,1)} %reshape.117), calls=%async_computation.1 | async-start | bytes 6291456 | tf_op jit(solution)/shard_map/all_to_all | solution.py:103
  98.2 0.6 copy-start.6
  148.7 9.4 %collective-permute-start.1 = (bf16[16,3,64,4]{2,0,3,1:T(8,128)(2,1)S(1)}, bf16[16,3,64,4]{2,0,3,1:T(8,128)(2,1)S(1)}, u32[]{:S(2)}, u32[]{:S(2)}) collective-permute-start(bf16[16,3,64,4]{2,0,3,1:T(8,128)(2,1)S(1)} %copy.44), channel_id=1, source_target_pairs={{32,0},{64,32},{96,64},{33,1},{65,33},{97,65},{34,2},{66,34},{98,6... | collective-permute-start | bytes 73736 | tf_op jit(solution)/shard_map/ppermute | solution.py:19
  152.0 4.8 %collective-permute-start = (bf16[16,3,64,4]{2,0,3,1:T(8,128)(2,1)S(1)}, bf16[16,3,64,4]{2,0,3,1:T(8,128)(2,1)S(1)}, u32[]{:S(2)}, u32[]{:S(2)}) collective-permute-start(bf16[16,3,64,4]{2,0,3,1:T(8,128)(2,1)S(1)} %copy.43), channel_id=1, source_target_pairs={{0,32},{32,64},{64,96},{1,33},{33,65},{65,97},{2,34},{34,66},{66,9... | collective-permute-start | bytes 73736 | tf_op jit(solution)/shard_map/ppermute | solution.py:18
  161.1 8.8 %collective-permute-start.2 = (bf16[16,3,4,520]{3,2,1,0:T(4,128)(2,1)S(1)}, bf16[16,3,4,520]{3,2,1,0:T(4,128)(2,1)S(1)}, u32[]{:S(2)}, u32[]{:S(2)}) collective-permute-start(bf16[16,3,4,520]{3,2,1,0:T(4,128)(2,1)S(1)} %get-tuple-element.126), channel_id=1, source_target_pairs={{0,1},{1,2},{2,3},{3,4},{4,5},{5,6},{6,7},{7,8},{8,9},{9,10},{10,1... | collective-permute-start | bytes 599048 | tf_op jit(solution)/shard_map/ppermute | solution.py:18
  166.7 8.9 %collective-permute-start.3 = (bf16[16,3,4,520]{3,2,1,0:T(4,128)(2,1)S(1)}, bf16[16,3,4,520]{3,2,1,0:T(4,128)(2,1)S(1)}, u32[]{:S(2)}, u32[]{:S(2)}) collective-permute-start(bf16[16,3,4,520]{3,2,1,0:T(4,128)(2,1)S(1)} %get-tuple-element.127), channel_id=1, source_target_pairs={{1,0},{2,1},{3,2},{4,3},{5,4},{6,5},{7,6},{8,7},{9,8},{10,9},{11,1... | collective-permute-start | bytes 599048 | tf_op jit(solution)/shard_map/ppermute | solution.py:19
  184.5 3.5 %copy-start.1 = (f32[3,8,64,512]{3,2,1,0:T(8,128)S(1)}, f32[3,8,64,512]{3,2,1,0:T(8,128)}, u32[]{:S(2)}) copy-start(f32[3,8,64,512]{3,2,1,0:T(8,128)} %param.15) | copy-start | bytes 9437188
  184.5 3.5 %copy-start.2 = (f32[3,64,512]{2,1,0:T(8,128)S(1)}, f32[3,64,512]{2,1,0:T(8,128)}, u32[]{:S(2)}) copy-start(f32[3,64,512]{2,1,0:T(8,128)} %param.14) | copy-start | bytes 1179652
  188.0 4.0 %copy-start.3 = (f32[64,512]{1,0:T(8,128)S(1)}, f32[64,512]{1,0:T(8,128)}, u32[]{:S(2)}) copy-start(f32[64,512]{1,0:T(8,128)} %get-tuple-element.280) | copy-start | bytes 393220 | tf_op jit(solution)/shard_map/while
  194.1 4.0 %copy-start.3 = (f32[64,512]{1,0:T(8,128)S(1)}, f32[64,512]{1,0:T(8,128)}, u32[]{:S(2)}) copy-start(f32[64,512]{1,0:T(8,128)} %get-tuple-element.280) | copy-start | bytes 393220 | tf_op jit(solution)/shard_map/while
  200.1 4.0 %copy-start.3 = (f32[64,512]{1,0:T(8,128)S(1)}, f32[64,512]{1,0:T(8,128)}, u32[]{:S(2)}) copy-start(f32[64,512]{1,0:T(8,128)} %get-tuple-element.280) | copy-start | bytes 393220 | tf_op jit(solution)/shard_map/while
  206.2 4.0 %copy-start.3 = (f32[64,512]{1,0:T(8,128)S(1)}, f32[64,512]{1,0:T(8,128)}, u32[]{:S(2)}) copy-start(f32[64,512]{1,0:T(8,128)} %get-tuple-element.280) | copy-start | bytes 393220 | tf_op jit(solution)/shard_map/while
  212.3 4.0 %copy-start.3 = (f32[64,512]{1,0:T(8,128)S(1)}, f32[64,512]{1,0:T(8,128)}, u32[]{:S(2)}) copy-start(f32[64,512]{1,0:T(8,128)} %get-tuple-element.280) | copy-start | bytes 393220 | tf_op jit(solution)/shard_map/while
  218.4 4.0 %copy-start.3 = (f32[64,512]{1,0:T(8,128)S(1)}, f32[64,512]{1,0:T(8,128)}, u32[]{:S(2)}) copy-start(f32[64,512]{1,0:T(8,128)} %get-tuple-element.280) | copy-start | bytes 393220 | tf_op jit(solution)/shard_map/while
  224.5 4.0 %copy-start.3 = (f32[64,512]{1,0:T(8,128)S(1)}, f32[64,512]{1,0:T(8,128)}, u32[]{:S(2)}) copy-start(f32[64,512]{1,0:T(8,128)} %get-tuple-element.280) | copy-start | bytes 393220 | tf_op jit(solution)/shard_map/while
  230.5 4.0 %copy-start.3 = (f32[64,512]{1,0:T(8,128)S(1)}, f32[64,512]{1,0:T(8,128)}, u32[]{:S(2)}) copy-start(f32[64,512]{1,0:T(8,128)} %get-tuple-element.280) | copy-start | bytes 393220 | tf_op jit(solution)/shard_map/while
  236.6 4.0 %copy-start.3 = (f32[64,512]{1,0:T(8,128)S(1)}, f32[64,512]{1,0:T(8,128)}, u32[]{:S(2)}) copy-start(f32[64,512]{1,0:T(8,128)} %get-tuple-element.280) | copy-start | bytes 393220 | tf_op jit(solution)/shard_map/while
  242.7 4.0 %copy-start.3 = (f32[64,512]{1,0:T(8,128)S(1)}, f32[64,512]{1,0:T(8,128)}, u32[]{:S(2)}) copy-start(f32[64,512]{1,0:T(8,128)} %get-tuple-element.280) | copy-start | bytes 393220 | tf_op jit(solution)/shard_map/while
  248.8 4.0 %copy-start.3 = (f32[64,512]{1,0:T(8,128)S(1)}, f32[64,512]{1,0:T(8,128)}, u32[]{:S(2)}) copy-start(f32[64,512]{1,0:T(8,128)} %get-tuple-element.280) | copy-start | bytes 393220 | tf_op jit(solution)/shard_map/while
  254.8 4.0 %copy-start.3 = (f32[64,512]{1,0:T(8,128)S(1)}, f32[64,512]{1,0:T(8,128)}, u32[]{:S(2)}) copy-start(f32[64,512]{1,0:T(8,128)} %get-tuple-element.280) | copy-start | bytes 393220 | tf_op jit(solution)/shard_map/while
  260.9 4.0 %copy-start.3 = (f32[64,512]{1,0:T(8,128)S(1)}, f32[64,512]{1,0:T(8,128)}, u32[]{:S(2)}) copy-start(f32[64,512]{1,0:T(8,128)} %get-tuple-element.280) | copy-start | bytes 393220 | tf_op jit(solution)/shard_map/while
  267.0 4.0 %copy-start.3 = (f32[64,512]{1,0:T(8,128)S(1)}, f32[64,512]{1,0:T(8,128)}, u32[]{:S(2)}) copy-start(f32[64,512]{1,0:T(8,128)} %get-tuple-element.280) | copy-start | bytes 393220 | tf_op jit(solution)/shard_map/while
  273.1 4.0 %copy-start.3 = (f32[64,512]{1,0:T(8,128)S(1)}, f32[64,512]{1,0:T(8,128)}, u32[]{:S(2)}) copy-start(f32[64,512]{1,0:T(8,128)} %get-tuple-element.280) | copy-start | bytes 393220 | tf_op jit(solution)/shard_map/while
  279.1 4.0 %copy-start.3 = (f32[64,512]{1,0:T(8,128)S(1)}, f32[64,512]{1,0:T(8,128)}, u32[]{:S(2)}) copy-start(f32[64,512]{1,0:T(8,128)} %get-tuple-element.280) | copy-start | bytes 393220 | tf_op jit(solution)/shard_map/while
  285.2 1.7 copy-start
